TPU v7x, 128 devices: a whole 4x4x4 slice. The times are simulated.
128 devices in a mesh: row: 8 (over x, core), col: 16 (over y, z).
Axes of the slice: x: 4, y: 4, z: 4, core: 2. Of those that a mesh axis runs over, the one named last changes fastest.
Arguments:
- panel_rows: float32 [8192, 4096], P('row', 'col'), may hold values from -0.75 to 0.75
- owner_slot: int32 [16, 16], replicated, may hold values from -1 to 31, as said below
Outputs:
- packed: float32 [8, 32, 512, 512], P('row', 'col')
Inputs may be any that keep to these rules, and one draw needn't show every extreme that they name: For j <= i, owner_slot[i, j] is the position of tile (i, j) among the 32 positions of group i // 2; tiles of one group have distinct positions; entries above the diagonal are -1. Position p lies on the device of col index p // 2.
All inputs are finite; a program needn't handle non-finite values.
Results may differ from a plain program's by a relative error of at most 0.0003.
Values sent between devices are 32-bit elements; how exact they have to be, the bound alone decides.
No kernel may reach another device: no remote copies, remote signals or barrier semaphores. Data moves between devices by JAX's collectives and lax.ppermute only.
A program may use at most 128 MiB of HBM per device.

v0:
```python
import jax
import jax.numpy as jnp
from jax import lax
from jax.sharding import PartitionSpec as P

BLOCK = 512


def slot_table(owner_slot, group_id, positions, per_group):
    blocks = owner_slot.shape[0]
    block_row = jnp.arange(blocks, dtype=jnp.int32)[:, None]
    block_col = jnp.arange(blocks, dtype=jnp.int32)[None, :]
    inside = (block_row // per_group == group_id) & (block_col <= block_row)
    wanted = jnp.arange(positions, dtype=jnp.int32)[:, None, None]
    matched = inside[None] & (owner_slot[None] == wanted)
    is_live = jnp.any(matched, axis=(1, 2))
    left_block = jnp.sum(jnp.where(matched, block_row[None], 0), axis=(1, 2))
    right_block = jnp.sum(jnp.where(matched, block_col[None], 0), axis=(1, 2))
    return (left_block, right_block, is_live)


def tile_products(tiles_all, lefts, rights, flags):

    def single(packed_item):
        left_one, right_one, flag = packed_item

        def compute():
            return lax.dot_general(
                tiles_all[left_one],
                tiles_all[right_one],
                (((1,), (1,)), ((), ())),
                precision=lax.Precision.HIGHEST,
                preferred_element_type=jnp.float32,
            )

        def blank():
            return jnp.zeros((BLOCK, BLOCK), jnp.float32)

        return lax.cond(flag, compute, blank)

    return lax.map(single, (lefts, rights, flags))


def body(panel_rows, owner_slot):
    rows_n = lax.axis_size("row")
    cols_n = lax.axis_size("col")
    slab_rows, inner_cols = panel_rows.shape
    per_group = slab_rows // BLOCK
    blocks = per_group * rows_n
    row_tiles = per_group * (blocks - per_group) + per_group * (per_group + 1) // 2
    slot_count = (row_tiles + cols_n - 1) // cols_n
    positions = cols_n * slot_count
    gathered = lax.all_gather(panel_rows, "row", axis=0, tiled=True)
    my_group = lax.axis_index("row")
    left_block, right_block, is_live = slot_table(owner_slot, my_group, positions, per_group)
    tiles_all = gathered.reshape(blocks, BLOCK, inner_cols)
    summed = lax.psum_scatter(
        tile_products(tiles_all, left_block, right_block, is_live),
        "col",
        scatter_dimension=0,
        tiled=True,
    )
    return summed[None]


def solution(mesh):
    placed = (P("row", "col"), P())
    return jax.shard_map(
        body, mesh=mesh, in_specs=placed, out_specs=P("row", "col", None, None), check_vma=False
    )
```

profile of v0, /device:TPU:1, one launch (start us, length us, event | category | flops | bytes accessed | tf_op | source)
XLA Modules:
  0.0 575.0 jit_solution(2577626217838474993)
XLA Ops:
  9.1 53.2 %all-gather.2.cloned.1.call-done = f32[8192,256]{1,0:T(8,128)} async-done(((f32[1024,256]{1,0:T(8,128)}), f32[8192,256]{1,0:T(8,128)}) %all-gather.2.cloned.1.call-update) | async-done | bytes 8388624 | tf_op jit(solution)/shard_map/all_gather | solution.py:53
  62.3 133.3 %while.10 = (s32[]{:T(128)}, f32[32,512,512]{2,1,0:T(8,128)}, pred[32]{0:T(512)(128)(4,1)S(1)}, s32[32]{0:T(128)S(1)}, f32[16,512,256]{2,1,0:T(8,128)}, /*index=5*/s32[32]{0:T(128)S(1)}, s32[]{:T(128)}) while((s32[]{:T(128)}, f32[32,512,512]{2,1,0:T(8,128)}, pred[32]{0:T(512)(128)(4,1)S(1)}, s32[32]{0:T(128)S(1)}, f32[16,512,256]{2,1,0:T(8,128)}, ...), condition=%wide.region_6.7_spmd, body=%wide.region_3.6_spmd.sunk | while | flops 805306368 | bytes 4195044 | solution.py:41
  63.6 7.6 %conditional.2 = (f32[1,512,512]{2,1,0:T(8,128)S(1)}) conditional(s32[]{:T(128)} %bitcast.14, () %tuple.31, (s32[32]{0:T(128)S(1)}, s32[]{:T(128)}, f32[16,512,256]{2,1,0:T(8,128)}, s32[32]{0:T(128)S(1)}) %tuple.32), branch_computations={%region_4.4_spmd, %region_5.5_spmd} | conditional | flops 805306368 | bytes 2097260 | solution.py:39
  69.0 2.2 convolution_bitcast_fusion
  71.2 1.1 constant_dynamic-update-slice_fusion.2
  73.7 1.1 constant_dynamic-update-slice_fusion.2
  76.3 1.1 constant_dynamic-update-slice_fusion.2
  78.8 1.1 constant_dynamic-update-slice_fusion.2
  81.4 1.0 constant_dynamic-update-slice_fusion.2
  83.9 1.1 constant_dynamic-update-slice_fusion.2
  86.3 7.6 %conditional.2 = (f32[1,512,512]{2,1,0:T(8,128)S(1)}) conditional(s32[]{:T(128)} %bitcast.14, () %tuple.31, (s32[32]{0:T(128)S(1)}, s32[]{:T(128)}, f32[16,512,256]{2,1,0:T(8,128)}, s32[32]{0:T(128)S(1)}) %tuple.32), branch_computations={%region_4.4_spmd, %region_5.5_spmd} | conditional | flops 805306368 | bytes 2097260 | solution.py:39
  91.6 2.2 convolution_bitcast_fusion
  93.9 1.1 constant_dynamic-update-slice_fusion.2
  96.4 1.0 constant_dynamic-update-slice_fusion.2
  98.8 7.6 %conditional.2 = (f32[1,512,512]{2,1,0:T(8,128)S(1)}) conditional(s32[]{:T(128)} %bitcast.14, () %tuple.31, (s32[32]{0:T(128)S(1)}, s32[]{:T(128)}, f32[16,512,256]{2,1,0:T(8,128)}, s32[32]{0:T(128)S(1)}) %tuple.32), branch_computations={%region_4.4_spmd, %region_5.5_spmd} | conditional | flops 805306368 | bytes 2097260 | solution.py:39
  104.1 2.2 convolution_bitcast_fusion
  106.4 1.1 constant_dynamic-update-slice_fusion.2
  109.0 1.0 constant_dynamic-update-slice_fusion.2
  111.5 1.1 constant_dynamic-update-slice_fusion.2
  114.0 1.0 constant_dynamic-update-slice_fusion.2
  116.5 1.1 constant_dynamic-update-slice_fusion.2
  119.1 1.0 constant_dynamic-update-slice_fusion.2
  121.6 1.1 constant_dynamic-update-slice_fusion.2
  124.1 1.1 constant_dynamic-update-slice_fusion.2
  126.7 1.1 constant_dynamic-update-slice_fusion.2
  129.2 1.1 constant_dynamic-update-slice_fusion.2
  131.8 1.1 constant_dynamic-update-slice_fusion.2
  134.3 1.1 constant_dynamic-update-slice_fusion.2
  136.7 7.6 %conditional.2 = (f32[1,512,512]{2,1,0:T(8,128)S(1)}) conditional(s32[]{:T(128)} %bitcast.14, () %tuple.31, (s32[32]{0:T(128)S(1)}, s32[]{:T(128)}, f32[16,512,256]{2,1,0:T(8,128)}, s32[32]{0:T(128)S(1)}) %tuple.32), branch_computations={%region_4.4_spmd, %region_5.5_spmd} | conditional | flops 805306368 | bytes 2097260 | solution.py:39
  142.0 2.2 convolution_bitcast_fusion
  144.3 1.1 constant_dynamic-update-slice_fusion.2
  146.6 7.6 %conditional.2 = (f32[1,512,512]{2,1,0:T(8,128)S(1)}) conditional(s32[]{:T(128)} %bitcast.14, () %tuple.31, (s32[32]{0:T(128)S(1)}, s32[]{:T(128)}, f32[16,512,256]{2,1,0:T(8,128)}, s32[32]{0:T(128)S(1)}) %tuple.32), branch_computations={%region_4.4_spmd, %region_5.5_spmd} | conditional | flops 805306368 | bytes 2097260 | solution.py:39
  152.0 2.2 convolution_bitcast_fusion
  154.2 1.1 constant_dynamic-update-slice_fusion.2
  156.8 1.1 constant_dynamic-update-slice_fusion.2
  159.2 7.6 %conditional.2 = (f32[1,512,512]{2,1,0:T(8,128)S(1)}) conditional(s32[]{:T(128)} %bitcast.14, () %tuple.31, (s32[32]{0:T(128)S(1)}, s32[]{:T(128)}, f32[16,512,256]{2,1,0:T(8,128)}, s32[32]{0:T(128)S(1)}) %tuple.32), branch_computations={%region_4.4_spmd, %region_5.5_spmd} | conditional | flops 805306368 | bytes 2097260 | solution.py:39
  164.5 2.2 convolution_bitcast_fusion
  166.8 1.1 constant_dynamic-update-slice_fusion.2
  169.3 1.1 constant_dynamic-update-slice_fusion.2
  171.9 1.0 constant_dynamic-update-slice_fusion.2
  174.4 1.0 constant_dynamic-update-slice_fusion.2
  179.4 1.1 constant_dynamic-update-slice_fusion.2
  182.0 1.0 constant_dynamic-update-slice_fusion.2
  184.5 1.1 constant_dynamic-update-slice_fusion.2
  186.9 7.6 %conditional.2 = (f32[1,512,512]{2,1,0:T(8,128)S(1)}) conditional(s32[]{:T(128)} %bitcast.14, () %tuple.31, (s32[32]{0:T(128)S(1)}, s32[]{:T(128)}, f32[16,512,256]{2,1,0:T(8,128)}, s32[32]{0:T(128)S(1)}) %tuple.32), branch_computations={%region_4.4_spmd, %region_5.5_spmd} | conditional | flops 805306368 | bytes 2097260 | solution.py:39
  192.2 2.2 convolution_bitcast_fusion
  194.5 1.1 constant_dynamic-update-slice_fusion.2
  195.6 372.5 %reduce-scatter.2.cloned.1.call-done = f32[2,512,512]{2,1,0:T(8,128)} async-done(((f32[32,512,512]{2,1,0:T(8,128)}), f32[2,512,512]{2,1,0:T(8,128)}) %reduce-scatter.2.cloned.1.call-update) | async-done | bytes 2097168 | tf_op jit(solution)/shard_map/reduce_scatter | solution.py:57
  (106 shorter events, 39.6 us)
Async XLA Ops:
  6.5 55.8 %all-gather.2.cloned.1.call-start = ((), (), s32[]{:S(2)}) async-start(), calls=%async_computation.1 | async-start | bytes 9437184 | tf_op jit(solution)/shard_map/all_gather | solution.py:53
  7.3 560.9 %reduce-scatter.2.cloned.1.call-start = ((), (), s32[]{:S(2)}) async-start(), calls=%async_computation.2 | async-start | bytes 35651584 | tf_op jit(solution)/shard_map/reduce_scatter | solution.py:57
Sparse Core Ops, SparseCore 0:
  9.0 53.2 all-gather.1
  195.7 372.3 reduce-scatter.1
where the time goes:
time: 578 us; the launch traced here: 575 us
  waiting for transfers between devices  426 us (74%)
  local copies, waits for them, and re-layouts  66.9 us (12%)
  loops' own time  50.8 us (9%)
  matrix products  15.6 us (3%)
  between operations  13.4 us (2%)
    reduce_scatter x1, waiting for transfers between devices, body(): lax.psum_scatter(tile_products(tiles_all, left_block, right_block, is_liv...  373 us
    all_gather x1, waiting for transfers between devices, body(): gathered = lax.all_gather(panel_rows, 'row', axis=0, tiled=True)  53.2 us
    dynamic_update_slice x32, local copies, waits for them, and re-layouts, tile_products(): return lax.map(single, (lefts, rights, flags))  34.3 us
    dynamic_slice x46, local copies, waits for them, and re-layouts, tile_products(): return lax.map(single, (lefts, rights, flags))  29.7 us
    another operation x32, loops' own time, single(): return lax.cond(flag, compute, blank)  28.9 us
    another operation x1, loops' own time, tile_products(): return lax.map(single, (lefts, rights, flags))  21.9 us
    dot_general x7, matrix products, compute(): lax.dot_general(tiles_all[left_one], tiles_all[right_one], (((1,), (1,)),...  15.6 us
  transfers between devices with their start and end apart: 2, of which 2 were waited for; matrix products, arithmetic and copies ran while one was open for 0% of the time, Pallas kernels for 0%

commit v1 on v0

--- a/solution.py
+++ b/solution.py
@@ -4,6 +4,34 @@
 from jax.sharding import PartitionSpec as P
 
 BLOCK = 512
+
+
+def apply_surface_now(values, join_dim):
+    values = jnp.moveaxis(values, 0, join_dim)
+    w2 = values.shape
+    v_next = values.reshape(*w2[:join_dim], w2[join_dim] * w2[join_dim + 1], *w2[join_dim + 2 :])
+    return v_next
+
+
+def grid_trace(state, ax_name):
+    front, w_next = (lax.axis_size(ax_name), lax.axis_index(ax_name))
+    newest, heard = (state[None], 1)
+    while heard < front:
+        arr_out = lax.ppermute(
+            newest, ax_name, list(map(lambda at: (at, at ^ heard), range(front)))
+        )
+        item_now = w_next & heard == 0
+        newest = jnp.concatenate(
+            [jnp.where(item_now, newest, arr_out), jnp.where(item_now, arr_out, newest)]
+        )
+        heard *= 2
+    return newest
+
+
+def mark_roads_on(block_here, sample, dim_i):
+    base_arr = grid_trace(block_here, sample)
+    big = apply_surface_now(base_arr, dim_i)
+    return big
 
 
 def slot_table(owner_slot, group_id, positions, per_group):
@@ -50,7 +78,7 @@
     row_tiles = per_group * (blocks - per_group) + per_group * (per_group + 1) // 2
     slot_count = (row_tiles + cols_n - 1) // cols_n
     positions = cols_n * slot_count
-    gathered = lax.all_gather(panel_rows, "row", axis=0, tiled=True)
+    gathered = mark_roads_on(panel_rows, "row", 0)
     my_group = lax.axis_index("row")
     left_block, right_block, is_live = slot_table(owner_slot, my_group, positions, per_group)
     tiles_all = gathered.reshape(blocks, BLOCK, inner_cols)

time: 578 us -> 673 us (1.16)
  waiting for transfers between devices: 426 us -> 507 us
  other arithmetic: 1.78 us -> 14.5 us
    ppermute x0 -> x3, waiting for transfers between devices: none -> 138 us  [grid_trace(): lax.ppermute(newest, ax_name, list(map(lambda at: (at, at ^ heard), range...]
    all_gather x1 -> x0, waiting for transfers between devices: 53.2 us -> none  [body(): gathered = lax.all_gather(panel_rows, 'row', axis=0, tiled=True)]
    select_n x0 -> x3, other arithmetic: none -> 7.35 us  [grid_trace(): jnp.where(item_now, newest, arr_out)]
    concatenate x0 -> x3, other arithmetic: none -> 6.81 us  [grid_trace(): jnp.concatenate([jnp.where(item_now, newest, arr_out), jnp.where(item_now...]
  transfers between devices with their start and end apart: 2 -> 4, of which waited for: 2 -> 4; matrix products, arithmetic and copies ran while one was open for 0% -> 0% of each run, Pallas kernels for 0% -> 0%
where the time goes in v1:
time: 673 us; the launch traced here: 670 us
  waiting for transfers between devices  507 us (75%)
  local copies, waits for them, and re-layouts  65 us (10%)
  loops' own time  49 us (7%)
  matrix products  15.6 us (2%)
  other arithmetic  14.5 us (2%)
  between operations  13.4 us (2%)
    reduce_scatter x1, waiting for transfers between devices, body(): lax.psum_scatter(tile_products(tiles_all, left_block, right_block, is_liv...  369 us
    ppermute x3, waiting for transfers between devices, grid_trace(): lax.ppermute(newest, ax_name, list(map(lambda at: (at, at ^ heard), range...  138 us
    dynamic_update_slice x32, local copies, waits for them, and re-layouts, tile_products(): return lax.map(single, (lefts, rights, flags))  34.1 us
    another operation x32, loops' own time, single(): return lax.cond(flag, compute, blank)  27.9 us
    dynamic_slice x46, local copies, waits for them, and re-layouts, tile_products(): return lax.map(single, (lefts, rights, flags))  26.9 us
    another operation x1, loops' own time, tile_products(): return lax.map(single, (lefts, rights, flags))  21.1 us
    dot_general x7, matrix products, compute(): lax.dot_general(tiles_all[left_one], tiles_all[right_one], (((1,), (1,)),...  15.6 us
  transfers between devices with their start and end apart: 4, of which 4 were waited for; matrix products, arithmetic and copies ran while one was open for 0% of the time, Pallas kernels for 0%

profile of v1, /device:TPU:1, one launch (start us, length us, event | category | flops | bytes accessed | tf_op | source)
XLA Modules:
  0.0 670.0 jit_solution(18443351076921023848)
XLA Ops:
  6.5 1.4 collective-permute-start
  7.9 2.5 collective-permute-done
  10.4 1.4 broadcast_select_fusion.5
  12.9 1.4 collective-permute-start.1
  14.3 45.6 %collective-permute-done.1 = f32[2,1024,256]{2,1,0:T(8,128)} collective-permute-done((f32[2,1024,256]{2,1,0:T(8,128)S(1)}, f32[2,1024,256]{2,1,0:T(8,128)}, u32[]{:S(2)}, u32[]{:S(2)}) %collective-permute-start.1) | collective-permute-done | bytes 2097184 | tf_op jit(solution)/shard_map/ppermute | solution.py:20
  59.9 2.1 broadcast_select_fusion.3
  62.1 2.5 pad_maximum_fusion.1
  64.7 2.9 collective-permute-start.2
  68.0 89.5 %collective-permute-done.2 = f32[4,1024,256]{2,1,0:T(8,128)} collective-permute-done((f32[4,1024,256]{2,1,0:T(8,128)}, f32[4,1024,256]{2,1,0:T(8,128)}, u32[]{:S(2)}, u32[]{:S(2)}) %collective-permute-start.2) | collective-permute-done | bytes 4194336 | tf_op jit(solution)/shard_map/ppermute | solution.py:20
  157.5 3.9 broadcast_select_fusion.1
  161.3 4.1 pad_maximum_fusion
  165.5 128.5 %while.10 = (s32[]{:T(128)}, f32[32,512,512]{2,1,0:T(8,128)}, pred[32]{0:T(512)(128)(4,1)S(1)}, s32[32]{0:T(128)S(1)}, f32[16,512,256]{2,1,0:T(8,128)}, /*index=5*/s32[32]{0:T(128)S(1)}, s32[]{:T(128)}) while((s32[]{:T(128)}, f32[32,512,512]{2,1,0:T(8,128)}, pred[32]{0:T(512)(128)(4,1)S(1)}, s32[32]{0:T(128)S(1)}, f32[16,512,256]{2,1,0:T(8,128)}, ...), condition=%wide.region_6.7_spmd, body=%wide.region_3.6_spmd.sunk | while | flops 805306368 | bytes 4195044 | solution.py:69
  166.7 7.3 %conditional.2 = (f32[1,512,512]{2,1,0:T(8,128)S(1)}) conditional(s32[]{:T(128)} %bitcast.17, () %tuple.34, (s32[32]{0:T(128)S(1)}, s32[]{:T(128)}, f32[16,512,256]{2,1,0:T(8,128)}, s32[32]{0:T(128)S(1)}) %tuple.35), branch_computations={%region_4.4_spmd, %region_5.5_spmd} | conditional | flops 805306368 | bytes 2097260 | solution.py:67
  171.8 2.2 convolution_bitcast_fusion
  176.4 1.1 constant_dynamic-update-slice_fusion.2
  178.9 1.1 constant_dynamic-update-slice_fusion.2
  181.4 1.1 constant_dynamic-update-slice_fusion.2
  183.8 1.1 constant_dynamic-update-slice_fusion.2
  186.2 1.1 constant_dynamic-update-slice_fusion.2
  188.5 7.3 %conditional.2 = (f32[1,512,512]{2,1,0:T(8,128)S(1)}) conditional(s32[]{:T(128)} %bitcast.17, () %tuple.34, (s32[32]{0:T(128)S(1)}, s32[]{:T(128)}, f32[16,512,256]{2,1,0:T(8,128)}, s32[32]{0:T(128)S(1)}) %tuple.35), branch_computations={%region_4.4_spmd, %region_5.5_spmd} | conditional | flops 805306368 | bytes 2097260 | solution.py:67
  193.6 2.2 convolution_bitcast_fusion
  195.9 1.1 constant_dynamic-update-slice_fusion.2
  198.3 1.1 constant_dynamic-update-slice_fusion.2
  200.6 7.3 %conditional.2 = (f32[1,512,512]{2,1,0:T(8,128)S(1)}) conditional(s32[]{:T(128)} %bitcast.17, () %tuple.34, (s32[32]{0:T(128)S(1)}, s32[]{:T(128)}, f32[16,512,256]{2,1,0:T(8,128)}, s32[32]{0:T(128)S(1)}) %tuple.35), branch_computations={%region_4.4_spmd, %region_5.5_spmd} | conditional | flops 805306368 | bytes 2097260 | solution.py:67
  205.7 2.2 convolution_bitcast_fusion
  208.0 1.1 constant_dynamic-update-slice_fusion.2
  217.7 1.1 constant_dynamic-update-slice_fusion.2
  222.6 1.1 constant_dynamic-update-slice_fusion.2
  229.9 1.1 constant_dynamic-update-slice_fusion.2
  232.4 1.1 constant_dynamic-update-slice_fusion.2
  234.8 1.1 constant_dynamic-update-slice_fusion.2
  237.1 7.3 %conditional.2 = (f32[1,512,512]{2,1,0:T(8,128)S(1)}) conditional(s32[]{:T(128)} %bitcast.17, () %tuple.34, (s32[32]{0:T(128)S(1)}, s32[]{:T(128)}, f32[16,512,256]{2,1,0:T(8,128)}, s32[32]{0:T(128)S(1)}) %tuple.35), branch_computations={%region_4.4_spmd, %region_5.5_spmd} | conditional | flops 805306368 | bytes 2097260 | solution.py:67
  242.2 2.2 convolution_bitcast_fusion
  244.5 1.1 constant_dynamic-update-slice_fusion.2
  246.8 7.3 %conditional.2 = (f32[1,512,512]{2,1,0:T(8,128)S(1)}) conditional(s32[]{:T(128)} %bitcast.17, () %tuple.34, (s32[32]{0:T(128)S(1)}, s32[]{:T(128)}, f32[16,512,256]{2,1,0:T(8,128)}, s32[32]{0:T(128)S(1)}) %tuple.35), branch_computations={%region_4.4_spmd, %region_5.5_spmd} | conditional | flops 805306368 | bytes 2097260 | solution.py:67
  251.8 2.2 convolution_bitcast_fusion
  254.1 1.1 constant_dynamic-update-slice_fusion.2
  256.5 1.1 constant_dynamic-update-slice_fusion.2
  258.8 7.3 %conditional.2 = (f32[1,512,512]{2,1,0:T(8,128)S(1)}) conditional(s32[]{:T(128)} %bitcast.17, () %tuple.34, (s32[32]{0:T(128)S(1)}, s32[]{:T(128)}, f32[16,512,256]{2,1,0:T(8,128)}, s32[32]{0:T(128)S(1)}) %tuple.35), branch_computations={%region_4.4_spmd, %region_5.5_spmd} | conditional | flops 805306368 | bytes 2097260 | solution.py:67
  263.9 2.2 convolution_bitcast_fusion
  266.2 1.1 constant_dynamic-update-slice_fusion.2
  268.6 1.1 constant_dynamic-update-slice_fusion.2
  278.4 1.1 constant_dynamic-update-slice_fusion.2
  283.3 1.1 constant_dynamic-update-slice_fusion.2
  285.6 7.3 %conditional.2 = (f32[1,512,512]{2,1,0:T(8,128)S(1)}) conditional(s32[]{:T(128)} %bitcast.17, () %tuple.34, (s32[32]{0:T(128)S(1)}, s32[]{:T(128)}, f32[16,512,256]{2,1,0:T(8,128)}, s32[32]{0:T(128)S(1)}) %tuple.35), branch_computations={%region_4.4_spmd, %region_5.5_spmd} | conditional | flops 805306368 | bytes 2097260 | solution.py:67
  290.7 2.2 convolution_bitcast_fusion
  292.9 1.1 constant_dynamic-update-slice_fusion.2
  294.0 369.2 %reduce-scatter.2.cloned.1.call-done = f32[2,512,512]{2,1,0:T(8,128)} async-done(((f32[32,512,512]{2,1,0:T(8,128)}), f32[2,512,512]{2,1,0:T(8,128)}) %reduce-scatter.2.cloned.1.call-update) | async-done | bytes 2097168 | tf_op jit(solution)/shard_map/reduce_scatter | solution.py:85
  (121 shorter events, 46.4 us)
Async XLA Ops:
  6.5 656.7 %reduce-scatter.2.cloned.1.call-start = ((), (), s32[]{:S(2)}) async-start(), calls=%async_computation.1 | async-start | bytes 35651584 | tf_op jit(solution)/shard_map/reduce_scatter | solution.py:85
  6.5 3.9 collective-permute-start
  11.8 1.0 copy-start.1
  12.9 47.0 %collective-permute-start.1 = (f32[2,1024,256]{2,1,0:T(8,128)S(1)}, f32[2,1024,256]{2,1,0:T(8,128)}, u32[]{:S(2)}, u32[]{:S(2)}) collective-permute-start(f32[2,1024,256]{2,1,0:T(8,128)S(1)} %pad_maximum_fusion.2), channel_id=1, source_target_pairs={{0,32},{16,48},{32,0},{48,16},{64,96},{80,112},{96,64},{112,80},{1... | collective-permute-start | bytes 6291464 | tf_op jit(solution)/shard_map/ppermute | solution.py:20
  62.0 2.7 copy-start
  62.0 5.6 copy-start.2
  64.7 92.7 %collective-permute-start.2 = (f32[4,1024,256]{2,1,0:T(8,128)}, f32[4,1024,256]{2,1,0:T(8,128)}, u32[]{:S(2)}, u32[]{:S(2)}) collective-permute-start(f32[4,1024,256]{2,1,0:T(8,128)} %pad_maximum_fusion.1), channel_id=1, source_target_pairs={{0,64},{16,80},{32,96},{48,112},{64,0},{80,16},{96,32},{112,48},{1... | collective-permute-start | bytes 12582920 | tf_op jit(solution)/shard_map/ppermute | solution.py:20
Sparse Core Ops, SparseCore 0:
  294.1 369.0 reduce-scatter.1
